TPU v7x, 8 devices: a whole 2x2x1 slice. The times are simulated.
8 devices in a mesh: rep: 2 (over z, y), fsdp: 4 (over x, core).
Axes of the slice: x: 2, y: 2, z: 1, core: 2. Of those that a mesh axis runs over, the one named last changes fastest.
Arguments:
- tokens: bfloat16 [8192, 2048], P(('rep', 'fsdp')), parts along dimension 0
- seg_ids: int32 [8192], P(('rep', 'fsdp')), parts along dimension 0
- w_q: bfloat16 [2, 2048, 2048], P(None, 'fsdp')
- w_k: bfloat16 [2, 2048, 256], P(None, 'fsdp')
- w_v: bfloat16 [2, 2048, 256], P(None, 'fsdp')
- w_o: bfloat16 [2, 2048, 2048], P(None, 'fsdp')
- w_gate: bfloat16 [2, 2048, 11008], P(None, 'fsdp')
- w_up: bfloat16 [2, 2048, 11008], P(None, 'fsdp')
- w_down: bfloat16 [2, 11008, 2048], P(None, 'fsdp')
- g_attn: bfloat16 [2, 2048], replicated
- g_mlp: bfloat16 [2, 2048], replicated
Outputs:
- output: float32 [8192, 2048], P(('rep', 'fsdp')), parts along dimension 0
There are 2 independent parts. A program takes and returns all parts, laid end to end along the dimension named above; an argument that names none is the same for every part.
All inputs are finite; a program needn't handle non-finite values.
Results may differ from a plain program's by a relative error of at most 0.0135712.
Values are sent between devices in bfloat16 or wider.
A program may use at most 1 GiB of HBM per device.

v0:
```python
import functools

import jax
import jax.numpy as jnp
import numpy as np
from jax import lax
from jax.experimental import pallas as pl
from jax.experimental.pallas import tpu as pltpu
from jax.sharding import PartitionSpec as P

D = 2048
FF = 11008
HEADS = 16
HEAD = 128
TOK = 1024
EPS = 1e-5
ROPE_BASE = 10000.0
MESH = pl.DeviceIdType.MESH
F32 = jnp.float32
BF16 = jnp.bfloat16

LAYERS = 2
SLOTS = 8
ITEM_SLOTS = 2 * SLOTS
AHEAD = 8
AHEAD0 = 5
ROWS = D // 4
FF_ROWS = FF // 4
TAIL = 192
NAMES = ("q", "k", "v", "o", "g", "u", "d")

N_Q = 4
N_GU = 21
N_D = 10
CH_Q = 1
CH_O = CH_Q + N_Q
CH_GU = CH_O + N_Q
CH_GL = CH_GU + N_GU
CH_D = CH_GL + 1
CH_DR = CH_D + N_D
PER_LAYER = CH_DR + 1
CHUNKS = LAYERS * PER_LAYER
ITEMS = 2 * CHUNKS
PUSHES = CHUNKS + 2

NEAR_AT = 5

N_GT = FF // 256
ST_Q = 1
ST_A = ST_Q + N_Q
ST_O = ST_A + HEADS
ST_G = ST_O + 4
ST_D = ST_G + N_GT
ST_NEAR = ST_D + 2 * NEAR_AT
ST_READY = ST_D + 2 * (N_D - 1)
ST_IDLE = ST_READY + 3
ST_FAR = ST_IDLE + 1
ST_REST = ST_FAR + 2
STEPS = ST_REST + 2
ALL_STEPS = LAYERS * STEPS - 2
START = (4, 1, 0)
FIRST = (8, 3, 1)
REST_K = 2 * TAIL
NEAR_K = 512 + REST_K

MB = 512
NB = 128
QB = 256


def layer_kernel(*refs):
    tok, seg, freq, g_attn, g_mlp = refs[:5]
    own = dict(zip(NAMES, refs[5:12]))
    x_ref, a_ref = refs[12:14]
    b1 = dict(zip(NAMES, refs[14:21]))
    b2 = dict(zip(NAMES, refs[21:28]))
    b3 = dict(zip(NAMES, refs[28:35]))
    (h_ref, q_ref, kv_ref, wbuf, dbuf, cos_ref, sin_ref, first_ref, gain_ref,
     seg_ref, freq_ref, ga_ref, gm_ref, wsem, dsem, iosem) = refs[35:51]
    s0s, s0r, s1s, s1r, s2s, s2r, s3s, s3r = refs[51:]
    sources = (own, b1, b2, b3)
    y = lax.axis_index("rep")
    d = lax.axis_index("fsdp")
    side = d // 2
    core = lax.rem(d, 2)
    x_dev = (y, lax.rem(d + 2, 4))
    y_dev = (1 - y, d)
    c_dev = (y, d + 1 - 2 * core)

    def rel(block):
        return 2 * lax.rem(block // 2 + side, 2) + lax.rem(block + core, 2)

    inputs = [pltpu.make_async_copy(src, dst, iosem.at[n]) for n, (src, dst) in enumerate(
        ((tok, q_ref), (seg, seg_ref), (freq, freq_ref), (g_attn, ga_ref), (g_mlp, gm_ref)))]
    for copy in inputs:
        copy.start()

    with jax.named_scope("barrier"):
        barrier = pltpu.get_barrier_semaphore()
        for dev in (x_dev, y_dev, c_dev):
            pl.semaphore_signal(barrier, inc=1, device_id=dev, device_id_type=MESH)
        pl.semaphore_wait(barrier, 3)

    def kinds(k):
        i = lax.rem(k, PER_LAYER)
        jq = pl.multiple_of((i - CH_Q) * 512, 512)
        jo = pl.multiple_of((i - CH_O) * 512, 512)
        jg = pl.multiple_of((i - CH_GU) * 512, 512)
        jd = core * TAIL + (i - CH_D) * 256
        jr = (1 - core) * 2560
        last = N_GU * 512
        kv = [("k", 0, ROWS, 0, 256), ("v", 0, ROWS, 0, 256)]
        gu = [("g", 0, ROWS, jg, 512), ("u", 0, ROWS, jg, 512)]
        gl = [("g", 0, ROWS, last, 256), ("u", 0, ROWS, last, 256)]

        def split_cols(name, c0):
            whole = [(name, 0, ROWS, c0, 512)]
            return [(name, 0, ROWS, c0, 256), (name, 0, ROWS, c0 + 256, 256)], whole, whole

        def split_rows(r0, nr):
            halves = [("d", r0, nr // 2, 0, D), ("d", r0 + nr // 2, nr // 2, 0, D)]
            return halves, [("d", r0, nr, 0, D)], halves

        return [
            (i == 0, kv, kv, kv),
            ((i >= CH_Q) & (i < CH_O), *split_cols("q", jq)),
            ((i >= CH_O) & (i < CH_GU), *split_cols("o", jo)),
            ((i >= CH_GU) & (i < CH_GL), gu, gu, gu),
            (i == CH_GL, gl, gl, gl),
            ((i >= CH_D) & (i < CH_DR), *split_rows(jd, 256)),
            (i == CH_DR, *split_rows(jr, TAIL)),
        ]

    def for_chunk(k, fn, form=2, part=None):
        layer = k // PER_LAYER
        slot = lax.rem(k, SLOTS)
        for kind in kinds(k):
            @pl.when((k < CHUNKS) & kind[0])
            def _():
                for n, piece in enumerate(kind[form]):
                    if part is None:
                        fn(False, layer, piece, (slot, n))
                    else:
                        @pl.when(part != 1 - n)
                        def _():
                            fn(False, layer, piece, (slot, n))

    def for_pair(k, fn, part=None):
        layer = k // PER_LAYER
        table = kinds(k)
        for c, (cond, pieces, _, _) in enumerate(table):
            for end in ((False, True) if c == len(table) - 1 else (None,)):
                here = cond if end is None else cond & ((k == CHUNKS - 1) if end else (k < CHUNKS - 1))

                @pl.when((k < CHUNKS) & here)
                def _():
                    for n, piece in enumerate(pieces):
                        args = (bool(end) and n == 1, layer, piece, (lax.rem(2 * k + n, ITEM_SLOTS),))
                        if part is None:
                            fn(*args)
                        else:
                            @pl.when(part != 1 - n)
                            def _():
                                fn(*args)

    def for_item(m, fn):
        k = m // 2
        n = lax.rem(m, 2)
        layer = k // PER_LAYER
        slot = (lax.rem(m, ITEM_SLOTS),)
        for cond, (one, two), _, _ in kinds(k):
            if one[0] == two[0]:
                name, r0, nr, c0, nc = one
                r0 = r0 + n * (nr if nc == D else 0)
                c0 = c0 + n * (0 if nc == D else nc) if nc == D else pl.multiple_of(c0 + n * nc, 256)
                piece = (name, r0, nr, c0 if nc != D else 0, nc)

                @pl.when((m < ITEMS - 1) & cond)
                def _():
                    fn(False, layer, piece, slot)
                if nc == D and nr == TAIL // 2:
                    @pl.when((m == ITEMS - 1) & cond)
                    def _():
                        fn(True, layer, piece, slot)
            else:
                for which, piece in enumerate((one, two)):
                    @pl.when((m < ITEMS) & cond & (n == which))
                    def _():
                        fn(False, layer, piece, slot)

    def view(bufs, name, layer, r0, nr, c0, nc, half):
        if half:
            nr = nr // 2
            r0 = r0 + y * nr
        r0 = pl.multiple_of(r0, 16)
        return bufs[name].at[layer, pl.ds(r0, nr), pl.ds(c0, nc)]

    def remote(src, dst, ss, rs, dev, half):
        def make(whole, layer, piece, slot):
            part = half and not whole
            return pltpu.make_async_remote_copy(
                src_ref=view(src, piece[0], layer, *piece[1:], part),
                dst_ref=view(dst, piece[0], layer, *piece[1:], part),
                send_sem=ss.at[slot], recv_sem=rs.at[slot], device_id=dev, device_id_type=MESH)
        return make

    copy0 = remote(own, b1, s0s, s0r, c_dev, False)
    copy1 = remote(own, b2, s1s, s1r, x_dev, True)
    copy2 = remote(b2, b2, s2s, s2r, y_dev, True)
    copy3 = remote(b2, b3, s3s, s3r, c_dev, False)

    def start0(*a):
        copy0(*a).start()

    def start1(*a):
        copy1(*a).start()

    def wait0(*a):
        copy0(*a).wait_recv()

    def relay2(*a):
        copy1(*a).wait_recv()
        if not a[0]:
            copy2(*a).start()

    def arrived(*a):
        if not a[0]:
            copy2(*a).wait_recv()
        copy1(*a).wait_send()

    def relay3(*a):
        copy3(*a).start()

    def pushed(*a):
        copy0(*a).wait_send()

    def finish(*a):
        copy3(*a).wait_recv()
        copy3(*a).wait_send()

    def sent(*a):
        if not a[0]:
            copy2(*a).wait_send()

    def targets(s):
        i = lax.rem(s, STEPS)
        layer = s // STEPS
        first = layer == 0
        late = 1 - jnp.minimum(layer, 1)
        t2 = jnp.where(i < ST_A, 9 + 2 * i + late,
             jnp.where(i < ST_G + 1, 18 + late + 3 * (i - ST_A) // 5,
             jnp.where(i < ST_D, jnp.maximum(i + 4, 31 + late + (i - ST_G - 1) // 2),
             jnp.where(i < ST_NEAR, jnp.maximum(i, ST_D + 3 + (2 * (i - ST_D) + 1) // 3),
             jnp.where(first, jnp.where(i < ST_NEAR + 2, i, jnp.where(i < ST_READY - 2, 40 + i // 2, jnp.where(i < ST_READY, i - 2, i - 3))),
             jnp.where(i < ST_READY - 2, 38 + (i + 1) // 2, 39 + i // 2))))))
        final = i == STEPS - 1
        t3 = jnp.where(i < ST_D, jnp.where(i < ST_A, 3 + i, (t2 - 3) // 2),
             jnp.where(first, jnp.where(i < ST_IDLE, (t2 - 2) // 2, CH_DR + (i - ST_IDLE + 1) // 2 + jnp.where(final, 1, 0)),
             jnp.where(i < ST_READY - 4, (t2 - 2) // 2, jnp.where(i < ST_READY + 2, 39 + (i - ST_READY + 4) // 3, i - ST_READY + 39 + jnp.where(i == ST_FAR, 1, 0)))))
        end = s >= ALL_STEPS - 2
        t2 = jnp.minimum(t2 + layer * 2 * PER_LAYER, jnp.where(end, ITEMS, ITEMS - 1))
        t3 = jnp.minimum(t3 + layer * PER_LAYER, PUSHES)
        nxt = jnp.minimum(s + 1, ALL_STEPS - 1)
        i = lax.rem(nxt, STEPS)
        base = nxt // STEPS * PER_LAYER
        done = jnp.where(i < ST_A, 1 + i,
               jnp.where(i < ST_O, ST_A,
               jnp.where(i < ST_G, 1 + CH_O + i - ST_O,
               jnp.where(i < ST_D, 1 + CH_GU + (i - ST_G) // 2,
               jnp.where(i < ST_NEAR, 1 + CH_D + (i - ST_D) // 2,
               jnp.where(i < ST_READY, CH_D + (i - ST_D) // 2,
               jnp.where(i < ST_READY + 1, CH_DR - 2,
               jnp.where(i < ST_FAR, CH_DR - 1,
               jnp.where(i < ST_REST, CH_DR, PER_LAYER)))))))))
        tf = jnp.maximum(jnp.minimum(t3 - 2, CHUNKS - 2), done + base)
        pushes = tf + jnp.where(tf == CHUNKS - 1, 1, 0)
        t3 = jnp.maximum(jnp.maximum(t3, pushes), base + jnp.where((i >= ST_READY) & (i < ST_FAR), CH_DR - 1, 0))
        return jnp.maximum(t2, 2 * jnp.minimum(t3, CHUNKS - 2)), t3, tf

    def relays(old, new):
        @pl.loop(old[0], new[0])
        def _(m):
            with jax.named_scope("r2"):
                for_item(m, relay2)
                for_item(m + AHEAD, start1)
                n = lax.rem(m, 2)
                for_chunk(m // 2 + jnp.where(n == 0, AHEAD0, CHUNKS), start0)
                for_chunk(m // 2 + jnp.where(n == 0, CHUNKS, AHEAD0 - 1), wait0)

        @pl.loop(old[1], new[1])
        def _(p):
            with jax.named_scope("r3"):
                extra = jnp.maximum(p - (CHUNKS - 2), 0)
                k = p - (extra + 1) // 2
                part = jnp.where(p < CHUNKS - 2, 2, lax.rem(extra, 2))
                for_pair(k, arrived, part)
                for_chunk(k, relay3, 3, part)
                for_chunk(jnp.where(part == 1, CHUNKS, k), pushed)

        @pl.loop(old[2], new[2])
        def _(k):
            with jax.named_scope("fin"):
                for_chunk(k, finish, 3)
                for_pair(k, sent)

    def down_step(i):
        n = i - ST_D - jnp.where(i > ST_READY, 1, 0) - jnp.where(i > ST_IDLE, 1, 0)
        j = n // 2
        near = (i >= ST_NEAR) & (i < ST_NEAR + 2)
        far = (i >= ST_FAR) & (i < ST_REST)
        rest = i >= ST_REST
        whole = (i >= ST_D) & (i < ST_IDLE) & ~near & (i != ST_READY)
        return j, jnp.where(i > ST_NEAR, j - 1, j), lax.rem(n + 2 * STEPS, 2), whole, near, far, rest

    def rest_col(side_no):
        return pl.multiple_of(side_no * (2 * FF_ROWS) + 2560, HEAD)

    def tile_col(side_no, core_no, tile):
        return pl.multiple_of(side_no * (2 * FF_ROWS) + core_no * (FF_ROWS + TAIL) + tile * 256, HEAD)

    def load_tile(s):
        layer = s // STEPS
        i = lax.rem(s, STEPS)
        slot = lax.rem(s, 2)

        def cols(name, c0, nc, w0):
            for r, src in enumerate(sources):
                pltpu.make_async_copy(src[name].at[layer, :, pl.ds(c0, nc)],
                                      wbuf.at[slot, pl.ds(r * ROWS, ROWS), pl.ds(w0, nc)], wsem.at[slot]).start()

        @pl.when(i == 0)
        def _():
            cols("k", 0, 256, 0)
            cols("v", 0, 256, 256)

        @pl.when((i >= ST_Q) & (i < ST_A))
        def _():
            cols("q", pl.multiple_of((i - ST_Q) * 512, 512), 512, 0)

        @pl.when((i >= ST_O) & (i < ST_G))
        def _():
            cols("o", pl.multiple_of((i - ST_O) * 512, 512), 512, 0)

        @pl.when((i >= ST_G) & (i < ST_D))
        def _():
            c0 = pl.multiple_of((i - ST_G) * 256, 256)
            cols("g", c0, 256, 0)
            cols("u", c0, 256, 256)

        j, tile, half, whole, near, far, rest = down_step(i)
        dslot = lax.rem(j + 2 * STEPS, 2)

        def rows_in(src, r0, nr, w0):
            pltpu.make_async_copy(src["d"].at[layer, pl.ds(r0, nr), :], dbuf.at[dslot, pl.ds(w0, nr), :], dsem.at[dslot]).start()

        def chunk_rows(r, tile_no, w0):
            src_core = core if r % 2 == 0 else 1 - core
            rows_in(sources[r], pl.multiple_of(src_core * TAIL + tile_no * 256, 64), 256, w0)

        def rest_rows(r, w0):
            src_core = core if r % 2 == 0 else 1 - core
            rows_in(sources[r], pl.multiple_of((1 - src_core) * 2560, 512), TAIL, pl.multiple_of(w0 + src_core * TAIL, 64))

        @pl.when((whole & (half == 0) & (i != ST_READY + 1)) | (i == ST_READY))
        def _():
            for r in range(3):
                chunk_rows(r, jnp.where(i == ST_READY, N_D - 2, tile), r * 256)

        @pl.when(whole & (half == 0))
        def _():
            chunk_rows(3, tile, 768)

        @pl.when(near & (half == 0))
        def _():
            for r in range(2):
                chunk_rows(r, N_D - 1, r * 256)
                rest_rows(r, 512)

        @pl.when(far & (half == 0))
        def _():
            for r in range(2):
                chunk_rows(2 + r, N_D - 1, r * 256)

        @pl.when(rest & (half == 0))
        def _():
            for r in range(2):
                rest_rows(2 + r, 0)

    def norm(layer, which):
        @pl.loop(0, TOK // NB)
        def _(m):
            rows = pl.ds(pl.multiple_of(m * NB, NB), NB)
            total = jnp.zeros((NB, 1), F32)
            for b in range(4):
                blk = x_ref[rows, pl.ds(b * ROWS, ROWS)]
                total = total + jnp.sum(blk * blk, axis=1, keepdims=True)
            inv = lax.rsqrt(total * (1.0 / D) + EPS)
            for b in range(4):
                blk = x_ref[rows, pl.ds(b * ROWS, ROWS)]
                gain = gain_ref[which * LAYERS + layer, :, pl.ds(b * ROWS, ROWS)]
                c0 = pl.multiple_of(rel(b) * ROWS, ROWS)
                h_ref[rows, pl.ds(c0, ROWS)] = (blk * inv * gain).astype(BF16)

    def rotate(vals, rows):
        vals = vals.astype(BF16).astype(F32)
        turned = pltpu.roll(vals, HEAD // 2, 1)
        return (vals * cos_ref[rows, :] + turned * sin_ref[rows, :]).astype(BF16)

    def tile_product(slot, finish_rows):
        @pl.loop(0, TOK // MB)
        def _(m):
            rows = pl.ds(pl.multiple_of(m * MB, MB), MB)
            finish_rows(rows, jnp.dot(h_ref[rows, :], wbuf[slot], preferred_element_type=F32))

    def kv_step(slot):
        def fin(rows, acc):
            for b in range(2):
                kv_ref[rows, pl.ds(b * HEAD, HEAD)] = rotate(acc[:, b * HEAD:(b + 1) * HEAD], rows)
            kv_ref[rows, pl.ds(256, 256)] = acc[:, 256:].astype(BF16)
        tile_product(slot, fin)

    def q_step(slot, j):
        def fin(rows, acc):
            for b in range(4):
                c0 = pl.multiple_of(j * 512 + b * HEAD, HEAD)
                q_ref[rows, pl.ds(c0, HEAD)] = rotate(acc[:, b * HEAD:(b + 1) * HEAD], rows)
        tile_product(slot, fin)

    def o_step(slot, j):
        def fin(rows, acc):
            c0 = pl.ds(pl.multiple_of(j * 512, 512), 512)
            x_ref[rows, c0] = x_ref[rows, c0] + acc
        tile_product(slot, fin)

    def g_step(slot, j):
        def fin(rows, acc):
            gate = acc[:, :256]
            up = acc[:, 256:]
            c0 = pl.multiple_of(j * 256, 256)
            a_ref[rows, pl.ds(c0, 256)] = (gate * jax.nn.sigmoid(gate) * up).astype(BF16)
        tile_product(slot, fin)

    def attend(head):
        kv = head // 8
        q0 = pl.multiple_of(head * HEAD, HEAD)
        k0 = pl.multiple_of(kv * HEAD, HEAD)
        v0 = pl.multiple_of(256 + kv * HEAD, HEAD)
        o0 = pl.multiple_of(rel(head // 4) * ROWS + lax.rem(head, 4) * HEAD, HEAD)
        scale = HEAD ** -0.5
        for b in range(TOK // QB):
            keys = (b + 1) * QB
            rows = pl.ds(b * QB, QB)
            scores = lax.dot_general(q_ref[rows, pl.ds(q0, HEAD)], kv_ref[pl.ds(0, keys), pl.ds(k0, HEAD)],
                                     (((1,), (1,)), ((), ())), preferred_element_type=F32)
            key_idx = lax.broadcasted_iota(jnp.int32, (QB, keys), 1)
            row_idx = lax.broadcasted_iota(jnp.int32, (QB, keys), 0) + b * QB
            first = jnp.concatenate([first_ref[rows, :]] * (keys // HEAD), axis=1)
            ok = (key_idx >= first) & (key_idx <= row_idx)
            scores = jnp.where(ok, scores, -1e30)
            top = jnp.max(scores, axis=1, keepdims=True)
            probs = jnp.exp((scores - top) * scale)
            inv = 1.0 / jnp.sum(probs, axis=1, keepdims=True)
            probs = (probs * inv).astype(BF16)
            mixed = jnp.dot(probs, kv_ref[pl.ds(0, keys), pl.ds(v0, HEAD)], preferred_element_type=F32)
            h_ref[rows, pl.ds(o0, HEAD)] = mixed.astype(BF16)

    def add_product(dslot, half, cols):
        rows = pl.ds(pl.multiple_of(half * MB, MB), MB)
        depth = sum(width for _, width in cols)
        lhs = jnp.concatenate([a_ref[rows, pl.ds(c0, width)] for c0, width in cols], axis=1)
        x_ref[rows, :] = x_ref[rows, :] + jnp.dot(lhs, dbuf[dslot, pl.ds(0, depth), :], preferred_element_type=F32)

    def wait_d(dslot, half, depth):
        @pl.when(half == 0)
        def _():
            part = dbuf.at[dslot, pl.ds(0, depth), :]
            pltpu.make_async_copy(part, part, dsem.at[dslot]).wait()

    def last_cols(side_no):
        return [(tile_col(side_no, core, N_D - 1), 256), (tile_col(side_no, 1 - core, N_D - 1), 256)]

    def wait_w(slot):
        pltpu.make_async_copy(wbuf.at[slot], wbuf.at[slot], wsem.at[slot]).wait()

    def step(s):
        before = [jnp.where(s == 0, one, two) for one, two in zip(FIRST, targets(s - 1))]
        relays(before, targets(s))

        @pl.when(s + 1 < ALL_STEPS)
        def _():
            load_tile(s + 1)

        with jax.named_scope("comp"):
            compute(s)

    def compute(s):
        layer = s // STEPS
        i = lax.rem(s, STEPS)
        slot = lax.rem(s, 2)

        @pl.when(((i == 0) & (layer > 0)) | (i == ST_G))
        def _():
            norm(layer, jnp.where(i == 0, 0, 1))

        @pl.when((i < ST_A) | ((i >= ST_O) & (i < ST_D)))
        def _():
            wait_w(slot)

        @pl.when(i == 0)
        def _():
            kv_step(slot)

        @pl.when((i >= ST_Q) & (i < ST_A))
        def _():
            q_step(slot, i - ST_Q)

        @pl.when((i >= ST_A) & (i < ST_O))
        def _():
            attend(i - ST_A)

        @pl.when((i >= ST_O) & (i < ST_G))
        def _():
            o_step(slot, i - ST_O)

        @pl.when((i >= ST_G) & (i < ST_D))
        def _():
            g_step(slot, i - ST_G)

        j, tile, half, whole, near, far, rest = down_step(i)
        dslot = lax.rem(j + 2 * STEPS, 2)

        @pl.when(whole)
        def _():
            wait_d(dslot, half, 1024)
            add_product(dslot, half, [(tile_col(lax.rem(side + r // 2, 2), lax.rem(core + r, 2), tile), 256) for r in range(4)])

        @pl.when(near)
        def _():
            wait_d(dslot, half, NEAR_K)
            add_product(dslot, half, last_cols(side) + [(rest_col(side), REST_K)])

        @pl.when(far)
        def _():
            wait_d(dslot, half, 512)
            add_product(dslot, half, last_cols(1 - side))

        @pl.when(rest)
        def _():
            wait_d(dslot, half, REST_K)
            add_product(dslot, half, [(rest_col(1 - side), REST_K)])

    @pl.loop(0, AHEAD)
    def _(m):
        for_item(m, start1)

    @pl.loop(0, AHEAD0)
    def _(k):
        for_chunk(k, start0)

    for copy in inputs:
        copy.wait()

    for n, ref in enumerate((ga_ref, gm_ref)):
        for layer in range(LAYERS):
            gain_ref[n * LAYERS + layer] = ref[pl.ds(layer, 1), :].astype(F32)
    ids = seg_ref[...].astype(F32)
    lane = lax.broadcasted_iota(jnp.int32, (128, HEAD), 1)
    for b in range(TOK // 128):
        rows = pl.ds(b * 128, 128)
        mine = jnp.transpose(jnp.broadcast_to(ids[b:b + 1, :], (128, 128)))
        before = jnp.zeros((128, 128), F32)
        for c in range(TOK // 128):
            before = before + jnp.where(ids[c:c + 1, :] < mine, 1.0, 0.0)
        first = jnp.sum(before, axis=1, keepdims=True)
        pos = lax.broadcasted_iota(jnp.int32, (128, 128), 0).astype(F32) + (b * 128.0) - first
        angles = pos * freq_ref[...]
        cos_ref[rows, :] = jnp.cos(angles)
        sin = jnp.sin(angles)
        sin_ref[rows, :] = jnp.where(lane < HEAD // 2, -sin, sin)
        first_ref[rows, :] = jnp.broadcast_to(first, (128, 128)).astype(jnp.int32)

    @pl.loop(0, TOK // NB)
    def _(m):
        rows = pl.ds(pl.multiple_of(m * NB, NB), NB)
        x_ref[rows, :] = q_ref[rows, :].astype(F32)

    relays((0, 0, 0), (2, 0, 0))
    norm(0, 0)

    @pl.loop(0, AHEAD0 - 1)
    def _(k):
        for_chunk(k, wait0)

    relays((2, 0, 0), START)
    relays(START, FIRST)
    load_tile(0)

    @pl.loop(0, ALL_STEPS)
    def _(s):
        with jax.named_scope("step"):
            step(s)

    relays(targets(ALL_STEPS - 1), (ITEMS, PUSHES, CHUNKS))


def result_kernel(x_ref, a_ref, w2_hbm, w3_hbm, out, y_ref, w_ref, wsem, osem):
    d = lax.axis_index("fsdp")
    core = lax.rem(d, 2)
    c0 = pl.multiple_of((1 - d // 2) * (2 * FF_ROWS) + 2560, HEAD)
    for n in range(4):
        cols = pl.ds(n * 512, 512)
        for src, src_core in ((w2_hbm, core), (w3_hbm, 1 - core)):
            r0 = pl.multiple_of((1 - src_core) * 2560, 512)
            d0 = pl.multiple_of(src_core * TAIL, 64)
            pltpu.make_async_copy(src.at[LAYERS - 1, pl.ds(r0, TAIL), cols], w_ref.at[n, pl.ds(d0, TAIL), :], wsem.at[n]).start()

    def store(n, m):
        rows, cols = pl.ds(m * 512, 512), pl.ds(n * 512, 512)
        return pltpu.make_async_copy(y_ref.at[rows, cols], out.at[rows, cols], osem.at[n, m])

    for n in range(4):
        cols = pl.ds(n * 512, 512)
        pltpu.make_async_copy(w_ref.at[n], w_ref.at[n], wsem.at[n]).wait()
        for m in range(2):
            rows = pl.ds(m * 512, 512)
            y_ref[rows, cols] = x_ref[rows, cols] + jnp.dot(a_ref[rows, pl.ds(c0, REST_K)], w_ref[n], preferred_element_type=F32)
            store(n, m).start()
    for n in range(4):
        for m in range(2):
            store(n, m).wait()


def run_layers(tokens, seg_ids, g_attn, g_mlp, weights):
    shapes = [jax.ShapeDtypeStruct(w.shape, w.dtype) for w in weights]
    half_dim = HEAD // 2
    freq = np.float32(ROPE_BASE) ** (-np.arange(half_dim, dtype=np.float32) / np.float32(half_dim))
    freq = jnp.asarray(np.concatenate([freq, freq]).reshape(1, HEAD))
    sem = pltpu.SemaphoreType.DMA((SLOTS, 2))
    item_sem = pltpu.SemaphoreType.DMA((ITEM_SLOTS,))
    any_spec = pl.BlockSpec(memory_space=pl.ANY)
    vmem_spec = pl.BlockSpec(memory_space=pltpu.VMEM)
    outs = pl.pallas_call(
        layer_kernel,
        out_shape=[pltpu.VMEM((TOK, D), F32), pltpu.VMEM((TOK, FF), BF16)] + shapes * 3,
        in_specs=[any_spec] * 12,
        out_specs=[vmem_spec] * 2 + [any_spec] * 21,
        scratch_shapes=[
            pltpu.VMEM((TOK, D), BF16),
            pltpu.VMEM((TOK, D), BF16),
            pltpu.VMEM((TOK, 512), BF16),
            pltpu.VMEM((2, D, 512), BF16),
            pltpu.VMEM((2, 1024, D), BF16),
            pltpu.VMEM((TOK, HEAD), F32),
            pltpu.VMEM((TOK, HEAD), F32),
            pltpu.VMEM((TOK, HEAD), jnp.int32),
            pltpu.VMEM((2 * LAYERS, 1, D), F32),
            pltpu.VMEM((TOK // 128, 128), jnp.int32),
            pltpu.VMEM((1, HEAD), F32),
            pltpu.VMEM((LAYERS, D), BF16),
            pltpu.VMEM((LAYERS, D), BF16),
            pltpu.SemaphoreType.DMA((2,)),
            pltpu.SemaphoreType.DMA((2,)),
            pltpu.SemaphoreType.DMA((5,)),
        ] + [sem] * 2 + [item_sem] * 4 + [sem] * 2,
        compiler_params=pltpu.CompilerParams(collective_id=0, has_side_effects=True, vmem_limit_bytes=34 * 1000 * 1000),
        name="two_layers",
    )(tokens, seg_ids.reshape(TOK // 128, 128), freq, g_attn, g_mlp, *weights)
    hidden = pltpu.with_memory_space_constraint(outs[0], pltpu.VMEM)
    act = pltpu.with_memory_space_constraint(outs[1], pltpu.VMEM)
    return pl.pallas_call(
        result_kernel,
        out_shape=jax.ShapeDtypeStruct((TOK, D), F32),
        in_specs=[vmem_spec] * 2 + [any_spec] * 2,
        out_specs=any_spec,
        scratch_shapes=[
            pltpu.VMEM((TOK, D), F32),
            pltpu.VMEM((4, REST_K, 512), BF16),
            pltpu.SemaphoreType.DMA((4,)),
            pltpu.SemaphoreType.DMA((4, 2)),
        ],
        compiler_params=pltpu.CompilerParams(vmem_limit_bytes=24 * 1000 * 1000),
        name="result",
    )(hidden, act, outs[15], outs[22])


def solution(mesh):
    tok_spec = P(("rep", "fsdp"), None)
    seg_spec = P(("rep", "fsdp"))
    mat_spec = P(None, "fsdp", None)
    gain_spec = P(None, None)

    def per_device(tokens, seg_ids, w_q, w_k, w_v, w_o, w_gate, w_up, w_down, g_attn, g_mlp):
        return run_layers(tokens, seg_ids, g_attn, g_mlp, (w_q, w_k, w_v, w_o, w_gate, w_up, w_down))

    return jax.shard_map(per_device, mesh=mesh, in_specs=(tok_spec, seg_spec, mat_spec, mat_spec, mat_spec, mat_spec, mat_spec, mat_spec, mat_spec, gain_spec, gain_spec), out_specs=tok_spec, check_vma=False)
```

profile of v0, /device:TPU:0, one launch (start us, length us, event | category | flops | bytes accessed | tf_op | source)
XLA Modules:
  0.0 845.0 jit_solution(3840612155857159073)
XLA Ops:
  0.0 839.8 %two_layers.1 = (f32[1024,2048]{1,0:T(8,128)S(1)}, bf16[1024,11008]{1,0:T(8,128)(2,1)S(1)}, bf16[2,512,2048]{2,1,0:T(8,128)(2,1)}, bf16[2,512,256]{2,1,0:T(8,128...) custom-call(bf16[1024,2048]{1,0:T(8,128)(2,1)} %refs_0_.1, ...), custom_call_target="tpu_custom_call" | custom-call | tf_op jit(solution)/shard_map/two_layers/pallas_call | solution.py:642
  839.8 5.0 result.1
where the time goes:
time: 845 us
  Pallas kernels  845 us (100%)
    pallas_call x1, Pallas kernels, run_layers(): pl.pallas_call(layer_kernel, out_shape=[pltpu.VMEM((TOK, D), F32), pltpu....  840 us

commit v1 on v0

--- a/solution.py
+++ b/solution.py
@@ -71,13 +71,13 @@
 def layer_kernel(*refs):
     tok, seg, freq, g_attn, g_mlp = refs[:5]
     own = dict(zip(NAMES, refs[5:12]))
-    x_ref, a_ref = refs[12:14]
-    b1 = dict(zip(NAMES, refs[14:21]))
-    b2 = dict(zip(NAMES, refs[21:28]))
-    b3 = dict(zip(NAMES, refs[28:35]))
+    x_ref, a_ref, rest_ref = refs[12:15]
+    b1 = dict(zip(NAMES, refs[15:22]))
+    b2 = dict(zip(NAMES, refs[22:29]))
+    b3 = dict(zip(NAMES, refs[29:36]))
     (h_ref, q_ref, kv_ref, wbuf, dbuf, cos_ref, sin_ref, first_ref, gain_ref,
-     seg_ref, freq_ref, ga_ref, gm_ref, wsem, dsem, iosem) = refs[35:51]
-    s0s, s0r, s1s, s1r, s2s, s2r, s3s, s3r = refs[51:]
+     seg_ref, freq_ref, ga_ref, gm_ref, far_ref, wsem, dsem, iosem, lsem) = refs[36:54]
+    s0s, s0r, s1s, s1r, s2s, s2r, s3s, s3r = refs[54:]
     sources = (own, b1, b2, b3)
     y = lax.axis_index("rep")
     d = lax.axis_index("fsdp")
@@ -122,13 +122,15 @@
             return halves, [("d", r0, nr, 0, D)], halves
 
         return [
-            (i == 0, kv, kv, kv),
-            ((i >= CH_Q) & (i < CH_O), *split_cols("q", jq)),
-            ((i >= CH_O) & (i < CH_GU), *split_cols("o", jo)),
-            ((i >= CH_GU) & (i < CH_GL), gu, gu, gu),
-            (i == CH_GL, gl, gl, gl),
-            ((i >= CH_D) & (i < CH_DR), *split_rows(jd, 256)),
-            (i == CH_DR, *split_rows(jr, TAIL)),
+            (i == 0, kv, kv, kv, 0),
+            ((i >= CH_Q) & (i < CH_O), *split_cols("q", jq), 0),
+            ((i >= CH_O) & (i < CH_GU), *split_cols("o", jo), 0),
+            ((i >= CH_GU) & (i < CH_GL), gu, gu, gu, 0),
+            (i == CH_GL, gl, gl, gl, 0),
+            ((i >= CH_D) & (i < CH_DR) & (k != CHUNKS - 2), *split_rows(jd, 256), 0),
+            (k == CHUNKS - 2, *split_rows(jd, 256), 2),
+            ((i == CH_DR) & (k != CHUNKS - 1), *split_rows(jr, TAIL), 0),
+            (k == CHUNKS - 1, *split_rows(jr, TAIL), 1),
         ]
 
     def for_chunk(k, fn, form=2, part=None):
@@ -139,54 +141,44 @@
             def _():
                 for n, piece in enumerate(kind[form]):
                     if part is None:
-                        fn(False, layer, piece, (slot, n))
+                        fn(kind[4], layer, piece, (slot, n))
                     else:
                         @pl.when(part != 1 - n)
                         def _():
-                            fn(False, layer, piece, (slot, n))
+                            fn(kind[4], layer, piece, (slot, n))
 
     def for_pair(k, fn, part=None):
         layer = k // PER_LAYER
-        table = kinds(k)
-        for c, (cond, pieces, _, _) in enumerate(table):
-            for end in ((False, True) if c == len(table) - 1 else (None,)):
-                here = cond if end is None else cond & ((k == CHUNKS - 1) if end else (k < CHUNKS - 1))
-
-                @pl.when((k < CHUNKS) & here)
-                def _():
-                    for n, piece in enumerate(pieces):
-                        args = (bool(end) and n == 1, layer, piece, (lax.rem(2 * k + n, ITEM_SLOTS),))
-                        if part is None:
+        for cond, pieces, _, _, mark in kinds(k):
+            @pl.when((k < CHUNKS) & cond)
+            def _():
+                for n, piece in enumerate(pieces):
+                    args = (mark == 1 and n == 1, layer, piece, (lax.rem(2 * k + n, ITEM_SLOTS),))
+                    if part is None:
+                        fn(*args)
+                    else:
+                        @pl.when(part != 1 - n)
+                        def _():
                             fn(*args)
-                        else:
-                            @pl.when(part != 1 - n)
-                            def _():
-                                fn(*args)
 
     def for_item(m, fn):
         k = m // 2
         n = lax.rem(m, 2)
         layer = k // PER_LAYER
         slot = (lax.rem(m, ITEM_SLOTS),)
-        for cond, (one, two), _, _ in kinds(k):
-            if one[0] == two[0]:
+        for cond, (one, two), _, _, mark in kinds(k):
+            if one[0] == two[0] and mark != 1:
                 name, r0, nr, c0, nc = one
-                r0 = r0 + n * (nr if nc == D else 0)
-                c0 = c0 + n * (0 if nc == D else nc) if nc == D else pl.multiple_of(c0 + n * nc, 256)
-                piece = (name, r0, nr, c0 if nc != D else 0, nc)
-
-                @pl.when((m < ITEMS - 1) & cond)
+                r0, c0 = (r0 + n * nr, c0) if nc == D else (r0, pl.multiple_of(c0 + n * nc, 256))
+
+                @pl.when((m < ITEMS) & cond)
                 def _():
-                    fn(False, layer, piece, slot)
-                if nc == D and nr == TAIL // 2:
-                    @pl.when((m == ITEMS - 1) & cond)
-                    def _():
-                        fn(True, layer, piece, slot)
+                    fn(False, layer, (name, r0, nr, c0, nc), slot)
             else:
                 for which, piece in enumerate((one, two)):
                     @pl.when((m < ITEMS) & cond & (n == which))
                     def _():
-                        fn(False, layer, piece, slot)
+                        fn(mark == 1 and which == 1, layer, piece, slot)
 
     def view(bufs, name, layer, r0, nr, c0, nc, half):
         if half:
@@ -207,7 +199,18 @@
     copy0 = remote(own, b1, s0s, s0r, c_dev, False)
     copy1 = remote(own, b2, s1s, s1r, x_dev, True)
     copy2 = remote(b2, b2, s2s, s2r, y_dev, True)
-    copy3 = remote(b2, b3, s3s, s3r, c_dev, False)
+
+    def copy3(mark, layer, piece, slot):
+        name, r0, nr, c0, nc = piece
+        if mark == 0:
+            return remote(b2, b3, s3s, s3r, c_dev, False)(False, layer, piece, slot)
+        if mark == 1:
+            dst = rest_ref.at[pl.ds(pl.multiple_of(r0 - (1 - core) * 2560 + core * TAIL, 32), nr), :]
+        else:
+            dst = far_ref.at[pl.ds(pl.multiple_of(r0 - core * TAIL - (N_D - 1) * 256 + 256, 128), nr), :]
+        return pltpu.make_async_remote_copy(
+            src_ref=view(b2, name, layer, r0, nr, c0, nc, False), dst_ref=dst,
+            send_sem=s3s.at[slot], recv_sem=s3r.at[slot], device_id=c_dev, device_id_type=MESH)
 
     def start0(*a):
         copy0(*a).start()
@@ -318,6 +321,15 @@
     def tile_col(side_no, core_no, tile):
         return pl.multiple_of(side_no * (2 * FF_ROWS) + core_no * (FF_ROWS + TAIL) + tile * 256, HEAD)
 
+    def near_far():
+        r0 = pl.multiple_of(core * TAIL + (N_D - 1) * 256, 64)
+        return pltpu.make_async_copy(b2["d"].at[LAYERS - 1, pl.ds(r0, 256), :], far_ref.at[pl.ds(0, 256), :], lsem.at[0])
+
+    def near_rest():
+        r0 = pl.multiple_of((1 - core) * 2560, 512)
+        return pltpu.make_async_copy(b2["d"].at[LAYERS - 1, pl.ds(r0, TAIL), :],
+                                     rest_ref.at[pl.ds(pl.multiple_of(core * TAIL, 64), TAIL), :], lsem.at[1])
+
     def load_tile(s):
         layer = s // STEPS
         i = lax.rem(s, STEPS)
@@ -376,10 +388,14 @@
                 chunk_rows(r, N_D - 1, r * 256)
                 rest_rows(r, 512)
 
-        @pl.when(far & (half == 0))
+        @pl.when(far & (half == 0) & (layer < LAYERS - 1))
         def _():
             for r in range(2):
                 chunk_rows(2 + r, N_D - 1, r * 256)
+
+        @pl.when(far & (half == 0) & (layer == LAYERS - 1))
+        def _():
+            near_far().start()
 
         @pl.when(rest & (half == 0))
         def _():
@@ -464,11 +480,12 @@
             mixed = jnp.dot(probs, kv_ref[pl.ds(0, keys), pl.ds(v0, HEAD)], preferred_element_type=F32)
             h_ref[rows, pl.ds(o0, HEAD)] = mixed.astype(BF16)
 
-    def add_product(dslot, half, cols):
+    def add_product(dslot, half, cols, tile_ref=None):
         rows = pl.ds(pl.multiple_of(half * MB, MB), MB)
         depth = sum(width for _, width in cols)
         lhs = jnp.concatenate([a_ref[rows, pl.ds(c0, width)] for c0, width in cols], axis=1)
-        x_ref[rows, :] = x_ref[rows, :] + jnp.dot(lhs, dbuf[dslot, pl.ds(0, depth), :], preferred_element_type=F32)
+        tile = dbuf[dslot, pl.ds(0, depth), :] if tile_ref is None else tile_ref[...]
+        x_ref[rows, :] = x_ref[rows, :] + jnp.dot(lhs, tile, preferred_element_type=F32)
 
     def wait_d(dslot, half, depth):
         @pl.when(half == 0)
@@ -539,10 +556,18 @@
             wait_d(dslot, half, NEAR_K)
             add_product(dslot, half, last_cols(side) + [(rest_col(side), REST_K)])
 
-        @pl.when(far)
+        @pl.when(far & (layer < LAYERS - 1))
         def _():
             wait_d(dslot, half, 512)
             add_product(dslot, half, last_cols(1 - side))
+
+        @pl.when(far & (layer == LAYERS - 1))
+        def _():
+            @pl.when(half == 0)
+            def _():
+                near_far().wait()
+                near_rest().start()
+            add_product(dslot, half, last_cols(1 - side), far_ref)
 
         @pl.when(rest)
         def _():
@@ -601,18 +626,11 @@
             step(s)
 
     relays(targets(ALL_STEPS - 1), (ITEMS, PUSHES, CHUNKS))
-
-
-def result_kernel(x_ref, a_ref, w2_hbm, w3_hbm, out, y_ref, w_ref, wsem, osem):
-    d = lax.axis_index("fsdp")
-    core = lax.rem(d, 2)
-    c0 = pl.multiple_of((1 - d // 2) * (2 * FF_ROWS) + 2560, HEAD)
-    for n in range(4):
-        cols = pl.ds(n * 512, 512)
-        for src, src_core in ((w2_hbm, core), (w3_hbm, 1 - core)):
-            r0 = pl.multiple_of((1 - src_core) * 2560, 512)
-            d0 = pl.multiple_of(src_core * TAIL, 64)
-            pltpu.make_async_copy(src.at[LAYERS - 1, pl.ds(r0, TAIL), cols], w_ref.at[n, pl.ds(d0, TAIL), :], wsem.at[n]).start()
+    near_rest().wait()
+
+
+def result_kernel(x_ref, a_ref, w_ref, out, y_ref, osem):
+    c0 = pl.multiple_of((1 - lax.axis_index("fsdp") // 2) * (2 * FF_ROWS) + 2560, HEAD)
 
     def store(n, m):
         rows, cols = pl.ds(m * 512, 512), pl.ds(n * 512, 512)
@@ -620,10 +638,9 @@
 
     for n in range(4):
         cols = pl.ds(n * 512, 512)
-        pltpu.make_async_copy(w_ref.at[n], w_ref.at[n], wsem.at[n]).wait()
         for m in range(2):
             rows = pl.ds(m * 512, 512)
-            y_ref[rows, cols] = x_ref[rows, cols] + jnp.dot(a_ref[rows, pl.ds(c0, REST_K)], w_ref[n], preferred_element_type=F32)
+            y_ref[rows, cols] = x_ref[rows, cols] + jnp.dot(a_ref[rows, pl.ds(c0, REST_K)], w_ref[:, cols], preferred_element_type=F32)
             store(n, m).start()
     for n in range(4):
         for m in range(2):
@@ -641,9 +658,9 @@
     vmem_spec = pl.BlockSpec(memory_space=pltpu.VMEM)
     outs = pl.pallas_call(
         layer_kernel,
-        out_shape=[pltpu.VMEM((TOK, D), F32), pltpu.VMEM((TOK, FF), BF16)] + shapes * 3,
+        out_shape=[pltpu.VMEM((TOK, D), F32), pltpu.VMEM((TOK, FF), BF16), pltpu.VMEM((REST_K, D), BF16)] + shapes * 3,
         in_specs=[any_spec] * 12,
-        out_specs=[vmem_spec] * 2 + [any_spec] * 21,
+        out_specs=[vmem_spec] * 3 + [any_spec] * 21,
         scratch_shapes=[
             pltpu.VMEM((TOK, D), BF16),
             pltpu.VMEM((TOK, D), BF16),
@@ -658,29 +675,30 @@
             pltpu.VMEM((1, HEAD), F32),
             pltpu.VMEM((LAYERS, D), BF16),
             pltpu.VMEM((LAYERS, D), BF16),
+            pltpu.VMEM((512, D), BF16),
             pltpu.SemaphoreType.DMA((2,)),
             pltpu.SemaphoreType.DMA((2,)),
             pltpu.SemaphoreType.DMA((5,)),
+            pltpu.SemaphoreType.DMA((2,)),
         ] + [sem] * 2 + [item_sem] * 4 + [sem] * 2,
-        compiler_params=pltpu.CompilerParams(collective_id=0, has_side_effects=True, vmem_limit_bytes=34 * 1000 * 1000),
+        compiler_params=pltpu.CompilerParams(collective_id=0, has_side_effects=True, vmem_limit_bytes=33 * 1000 * 1000),
         name="two_layers",
     )(tokens, seg_ids.reshape(TOK // 128, 128), freq, g_attn, g_mlp, *weights)
     hidden = pltpu.with_memory_space_constraint(outs[0], pltpu.VMEM)
     act = pltpu.with_memory_space_constraint(outs[1], pltpu.VMEM)
+    rest = pltpu.with_memory_space_constraint(outs[2], pltpu.VMEM)
     return pl.pallas_call(
         result_kernel,
         out_shape=jax.ShapeDtypeStruct((TOK, D), F32),
-        in_specs=[vmem_spec] * 2 + [any_spec] * 2,
+        in_specs=[vmem_spec] * 3,
         out_specs=any_spec,
         scratch_shapes=[
             pltpu.VMEM((TOK, D), F32),
-            pltpu.VMEM((4, REST_K, 512), BF16),
-            pltpu.SemaphoreType.DMA((4,)),
             pltpu.SemaphoreType.DMA((4, 2)),
         ],
         compiler_params=pltpu.CompilerParams(vmem_limit_bytes=24 * 1000 * 1000),
         name="result",
-    )(hidden, act, outs[15], outs[22])
+    )(hidden, act, rest)
 
 
 def solution(mesh):

time: 845 us -> 866 us (1.025)
  local copies, waits for them, and re-layouts: 0 us -> 21.7 us
    unnamed x0 -> x8, local copies, waits for them, and re-layouts: none -> 21.7 us
where the time goes in v1:
time: 866 us
  Pallas kernels  844 us (97%)
  local copies, waits for them, and re-layouts  21.7 us (3%)
    pallas_call x1, Pallas kernels, run_layers(): pl.pallas_call(layer_kernel, out_shape=[pltpu.VMEM((TOK, D), F32), pltpu....  840 us
    unnamed x8, local copies, waits for them, and re-layouts  21.7 us

profile of v1, /device:TPU:0, one launch (start us, length us, event | category | flops | bytes accessed | tf_op | source)
XLA Modules:
  0.0 865.6 jit_solution(721692479309681895)
XLA Ops:
  0.0 839.9 %two_layers.1 = (f32[1024,2048]{1,0:T(8,128)S(1)}, bf16[1024,11008]{1,0:T(8,128)(2,1)S(1)}, bf16[384,2048]{1,0:T(8,128)(2,1)S(1)}, bf16[2,512,2048]{2,1,0:T(8,12...) custom-call(bf16[1024,2048]{1,0:T(8,128)(2,1)} %refs_0_.1, ...), custom_call_target="tpu_custom_call" | custom-call | tf_op jit(solution)/shard_map/two_layers/pallas_call | solution.py:659
  839.9 0.0 copy-start
  839.9 7.5 copy-done
  847.4 0.0 copy-start.2
  847.4 3.4 copy-done.2
  850.8 0.0 copy-start.1
  850.8 7.4 copy-done.1
  858.2 0.0 copy-start.3
  858.2 3.4 copy-done.3
  861.6 3.8 result.1
Async XLA Ops:
  839.9 7.5 copy-start
  847.4 3.4 copy-start.2
  850.8 7.4 copy-start.1
  858.2 3.4 copy-start.3

commit v2 on v1

--- a/solution.py
+++ b/solution.py
@@ -41,7 +41,7 @@
 PER_LAYER = CH_DR + 1
 CHUNKS = LAYERS * PER_LAYER
 ITEMS = 2 * CHUNKS
-PUSHES = CHUNKS + 2
+PUSHES = CHUNKS + 1
 
 NEAR_AT = 5
 
@@ -61,6 +61,7 @@
 START = (4, 1, 0)
 FIRST = (8, 3, 1)
 REST_K = 2 * TAIL
+WIDE = D // 2
 NEAR_K = 512 + REST_K
 
 MB = 512
@@ -71,13 +72,13 @@
 def layer_kernel(*refs):
     tok, seg, freq, g_attn, g_mlp = refs[:5]
     own = dict(zip(NAMES, refs[5:12]))
-    x_ref, a_ref, rest_ref = refs[12:15]
-    b1 = dict(zip(NAMES, refs[15:22]))
-    b2 = dict(zip(NAMES, refs[22:29]))
-    b3 = dict(zip(NAMES, refs[29:36]))
+    x_ref, a_ref = refs[12:14]
+    b1 = dict(zip(NAMES, refs[14:21]))
+    b2 = dict(zip(NAMES, refs[21:28]))
+    b3 = dict(zip(NAMES, refs[28:35]))
     (h_ref, q_ref, kv_ref, wbuf, dbuf, cos_ref, sin_ref, first_ref, gain_ref,
-     seg_ref, freq_ref, ga_ref, gm_ref, far_ref, wsem, dsem, iosem, lsem) = refs[36:54]
-    s0s, s0r, s1s, s1r, s2s, s2r, s3s, s3r = refs[54:]
+     seg_ref, freq_ref, ga_ref, gm_ref, far_ref, wsem, dsem, iosem, lsem) = refs[35:53]
+    s0s, s0r, s1s, s1r, s2s, s2r, s3s, s3r = refs[53:]
     sources = (own, b1, b2, b3)
     y = lax.axis_index("rep")
     d = lax.axis_index("fsdp")
@@ -130,7 +131,7 @@
             ((i >= CH_D) & (i < CH_DR) & (k != CHUNKS - 2), *split_rows(jd, 256), 0),
             (k == CHUNKS - 2, *split_rows(jd, 256), 2),
             ((i == CH_DR) & (k != CHUNKS - 1), *split_rows(jr, TAIL), 0),
-            (k == CHUNKS - 1, *split_rows(jr, TAIL), 1),
+            (k == CHUNKS - 1, *split_rows(jr, TAIL)[:2], [("d", jr, TAIL, 0, WIDE), ("d", jr, TAIL, WIDE, WIDE)], 1),
         ]
 
     def for_chunk(k, fn, form=2, part=None):
@@ -200,12 +201,15 @@
     copy1 = remote(own, b2, s1s, s1r, x_dev, True)
     copy2 = remote(b2, b2, s2s, s2r, y_dev, True)
 
+    def rest_rows(c0):
+        return a_ref.at[pl.ds(pl.multiple_of(c0 // WIDE * REST_K + core * TAIL, 64), TAIL), pl.ds(FF, WIDE)]
+
     def copy3(mark, layer, piece, slot):
         name, r0, nr, c0, nc = piece
         if mark == 0:
             return remote(b2, b3, s3s, s3r, c_dev, False)(False, layer, piece, slot)
         if mark == 1:
-            dst = rest_ref.at[pl.ds(pl.multiple_of(r0 - (1 - core) * 2560 + core * TAIL, 32), nr), :]
+            dst = rest_rows(c0)
         else:
             dst = far_ref.at[pl.ds(pl.multiple_of(r0 - core * TAIL - (N_D - 1) * 256 + 256, 128), nr), :]
         return pltpu.make_async_remote_copy(
@@ -294,8 +298,8 @@
         def _(p):
             with jax.named_scope("r3"):
                 extra = jnp.maximum(p - (CHUNKS - 2), 0)
-                k = p - (extra + 1) // 2
-                part = jnp.where(p < CHUNKS - 2, 2, lax.rem(extra, 2))
+                k = p - jnp.minimum(extra, 1)
+                part = jnp.where((p < CHUNKS - 2) | (extra > 1), 2, extra)
                 for_pair(k, arrived, part)
                 for_chunk(k, relay3, 3, part)
                 for_chunk(jnp.where(part == 1, CHUNKS, k), pushed)
@@ -327,8 +331,8 @@
 
     def near_rest():
         r0 = pl.multiple_of((1 - core) * 2560, 512)
-        return pltpu.make_async_copy(b2["d"].at[LAYERS - 1, pl.ds(r0, TAIL), :],
-                                     rest_ref.at[pl.ds(pl.multiple_of(core * TAIL, 64), TAIL), :], lsem.at[1])
+        return [pltpu.make_async_copy(b2["d"].at[LAYERS - 1, pl.ds(r0, TAIL), pl.ds(n * WIDE, WIDE)], rest_rows(n * WIDE), lsem.at[1 + n])
+                for n in range(2)]
 
     def load_tile(s):
         layer = s // STEPS
@@ -566,7 +570,8 @@
             @pl.when(half == 0)
             def _():
                 near_far().wait()
-                near_rest().start()
+                for copy in near_rest():
+                    copy.start()
             add_product(dslot, half, last_cols(1 - side), far_ref)
 
         @pl.when(rest)
@@ -626,10 +631,11 @@
             step(s)
 
     relays(targets(ALL_STEPS - 1), (ITEMS, PUSHES, CHUNKS))
-    near_rest().wait()
-
-
-def result_kernel(x_ref, a_ref, w_ref, out, y_ref, osem):
+    for copy in near_rest():
+        copy.wait()
+
+
+def result_kernel(x_ref, a_ref, out, y_ref, osem):
     c0 = pl.multiple_of((1 - lax.axis_index("fsdp") // 2) * (2 * FF_ROWS) + 2560, HEAD)
 
     def store(n, m):
@@ -638,9 +644,10 @@
 
     for n in range(4):
         cols = pl.ds(n * 512, 512)
+        tile = a_ref[pl.ds(n // 2 * REST_K, REST_K), pl.ds(FF + n % 2 * 512, 512)]
         for m in range(2):
             rows = pl.ds(m * 512, 512)
-            y_ref[rows, cols] = x_ref[rows, cols] + jnp.dot(a_ref[rows, pl.ds(c0, REST_K)], w_ref[:, cols], preferred_element_type=F32)
+            y_ref[rows, cols] = x_ref[rows, cols] + jnp.dot(a_ref[rows, pl.ds(c0, REST_K)], tile, preferred_element_type=F32)
             store(n, m).start()
     for n in range(4):
         for m in range(2):
@@ -658,9 +665,9 @@
     vmem_spec = pl.BlockSpec(memory_space=pltpu.VMEM)
     outs = pl.pallas_call(
         layer_kernel,
-        out_shape=[pltpu.VMEM((TOK, D), F32), pltpu.VMEM((TOK, FF), BF16), pltpu.VMEM((REST_K, D), BF16)] + shapes * 3,
+        out_shape=[pltpu.VMEM((TOK, D), F32), pltpu.VMEM((TOK, FF + WIDE), BF16)] + shapes * 3,
         in_specs=[any_spec] * 12,
-        out_specs=[vmem_spec] * 3 + [any_spec] * 21,
+        out_specs=[vmem_spec] * 2 + [any_spec] * 21,
         scratch_shapes=[
             pltpu.VMEM((TOK, D), BF16),
             pltpu.VMEM((TOK, D), BF16),
@@ -679,18 +686,17 @@
             pltpu.SemaphoreType.DMA((2,)),
             pltpu.SemaphoreType.DMA((2,)),
             pltpu.SemaphoreType.DMA((5,)),
-            pltpu.SemaphoreType.DMA((2,)),
+            pltpu.SemaphoreType.DMA((3,)),
         ] + [sem] * 2 + [item_sem] * 4 + [sem] * 2,
-        compiler_params=pltpu.CompilerParams(collective_id=0, has_side_effects=True, vmem_limit_bytes=33 * 1000 * 1000),
+        compiler_params=pltpu.CompilerParams(collective_id=0, has_side_effects=True, vmem_limit_bytes=32 * 1000 * 1000),
         name="two_layers",
     )(tokens, seg_ids.reshape(TOK // 128, 128), freq, g_attn, g_mlp, *weights)
     hidden = pltpu.with_memory_space_constraint(outs[0], pltpu.VMEM)
     act = pltpu.with_memory_space_constraint(outs[1], pltpu.VMEM)
-    rest = pltpu.with_memory_space_constraint(outs[2], pltpu.VMEM)
     return pl.pallas_call(
         result_kernel,
         out_shape=jax.ShapeDtypeStruct((TOK, D), F32),
-        in_specs=[vmem_spec] * 3,
+        in_specs=[vmem_spec] * 2,
         out_specs=any_spec,
         scratch_shapes=[
             pltpu.VMEM((TOK, D), F32),
@@ -698,7 +704,7 @@
         ],
         compiler_params=pltpu.CompilerParams(vmem_limit_bytes=24 * 1000 * 1000),
         name="result",
-    )(hidden, act, rest)
+    )(hidden, act)
 
 
 def solution(mesh):

time: 866 us -> 844 us (0.975)
  local copies, waits for them, and re-layouts: 21.7 us -> 0 us
    unnamed x8 -> x0, local copies, waits for them, and re-layouts: 21.7 us -> none
where the time goes in v2:
time: 844 us
  Pallas kernels  844 us (100%)
    pallas_call x1, Pallas kernels, run_layers(): pl.pallas_call(layer_kernel, out_shape=[pltpu.VMEM((TOK, D), F32), pltpu....  840 us

profile of v2, /device:TPU:0, one launch (start us, length us, event | category | flops | bytes accessed | tf_op | source)
XLA Modules:
  0.0 843.9 jit_solution(8806825129882852611)
XLA Ops:
  0.0 839.9 %two_layers.1 = (f32[1024,2048]{1,0:T(8,128)S(1)}, bf16[1024,12032]{1,0:T(8,128)(2,1)S(1)}, bf16[2,512,2048]{2,1,0:T(8,128)(2,1)}, bf16[2,512,256]{2,1,0:T(8,128...) custom-call(bf16[1024,2048]{1,0:T(8,128)(2,1)} %refs_0_.1, ...), custom_call_target="tpu_custom_call" | custom-call | tf_op jit(solution)/shard_map/two_layers/pallas_call | solution.py:666
  839.9 3.8 result.1

commit v3 on v2

--- a/solution.py
+++ b/solution.py
@@ -9,9 +9,12 @@
 from jax.sharding import PartitionSpec as P
 
 D = 2048
+WIDTH = 512
+PART = 256
+LANES = 128
 FF = 11008
 HEADS = 16
-HEAD = 128
+HEAD = LANES
 TOK = 1024
 EPS = 1e-5
 ROPE_BASE = 10000.0
@@ -45,7 +48,7 @@
 
 NEAR_AT = 5
 
-N_GT = FF // 256
+N_GT = FF // PART
 ST_Q = 1
 ST_A = ST_Q + N_Q
 ST_O = ST_A + HEADS
@@ -62,11 +65,11 @@
 FIRST = (8, 3, 1)
 REST_K = 2 * TAIL
 WIDE = D // 2
-NEAR_K = 512 + REST_K
-
-MB = 512
-NB = 128
-QB = 256
+NEAR_K = WIDTH + REST_K
+
+MB = WIDTH
+NB = LANES
+QB = PART
 
 
 def layer_kernel(*refs):
@@ -104,19 +107,19 @@
 
     def kinds(k):
         i = lax.rem(k, PER_LAYER)
-        jq = pl.multiple_of((i - CH_Q) * 512, 512)
-        jo = pl.multiple_of((i - CH_O) * 512, 512)
-        jg = pl.multiple_of((i - CH_GU) * 512, 512)
-        jd = core * TAIL + (i - CH_D) * 256
+        jq = pl.multiple_of((i - CH_Q) * WIDTH, WIDTH)
+        jo = pl.multiple_of((i - CH_O) * WIDTH, WIDTH)
+        jg = pl.multiple_of((i - CH_GU) * WIDTH, WIDTH)
+        jd = core * TAIL + (i - CH_D) * PART
         jr = (1 - core) * 2560
-        last = N_GU * 512
-        kv = [("k", 0, ROWS, 0, 256), ("v", 0, ROWS, 0, 256)]
-        gu = [("g", 0, ROWS, jg, 512), ("u", 0, ROWS, jg, 512)]
-        gl = [("g", 0, ROWS, last, 256), ("u", 0, ROWS, last, 256)]
+        last = N_GU * WIDTH
+        kv = [("k", 0, ROWS, 0, PART), ("v", 0, ROWS, 0, PART)]
+        gu = [("g", 0, ROWS, jg, WIDTH), ("u", 0, ROWS, jg, WIDTH)]
+        gl = [("g", 0, ROWS, last, PART), ("u", 0, ROWS, last, PART)]
 
         def split_cols(name, c0):
-            whole = [(name, 0, ROWS, c0, 512)]
-            return [(name, 0, ROWS, c0, 256), (name, 0, ROWS, c0 + 256, 256)], whole, whole
+            whole = [(name, 0, ROWS, c0, WIDTH)]
+            return [(name, 0, ROWS, c0, PART), (name, 0, ROWS, c0 + PART, PART)], whole, whole
 
         def split_rows(r0, nr):
             halves = [("d", r0, nr // 2, 0, D), ("d", r0 + nr // 2, nr // 2, 0, D)]
@@ -128,8 +131,8 @@
             ((i >= CH_O) & (i < CH_GU), *split_cols("o", jo), 0),
             ((i >= CH_GU) & (i < CH_GL), gu, gu, gu, 0),
             (i == CH_GL, gl, gl, gl, 0),
-            ((i >= CH_D) & (i < CH_DR) & (k != CHUNKS - 2), *split_rows(jd, 256), 0),
-            (k == CHUNKS - 2, *split_rows(jd, 256), 2),
+            ((i >= CH_D) & (i < CH_DR) & (k != CHUNKS - 2), *split_rows(jd, PART), 0),
+            (k == CHUNKS - 2, *split_rows(jd, PART), 2),
             ((i == CH_DR) & (k != CHUNKS - 1), *split_rows(jr, TAIL), 0),
             (k == CHUNKS - 1, *split_rows(jr, TAIL)[:2], [("d", jr, TAIL, 0, WIDE), ("d", jr, TAIL, WIDE, WIDE)], 1),
         ]
@@ -170,7 +173,7 @@
         for cond, (one, two), _, _, mark in kinds(k):
             if one[0] == two[0] and mark != 1:
                 name, r0, nr, c0, nc = one
-                r0, c0 = (r0 + n * nr, c0) if nc == D else (r0, pl.multiple_of(c0 + n * nc, 256))
+                r0, c0 = (r0 + n * nr, c0) if nc == D else (r0, pl.multiple_of(c0 + n * nc, PART))
 
                 @pl.when((m < ITEMS) & cond)
                 def _():
@@ -211,7 +214,7 @@
         if mark == 1:
             dst = rest_rows(c0)
         else:
-            dst = far_ref.at[pl.ds(pl.multiple_of(r0 - core * TAIL - (N_D - 1) * 256 + 256, 128), nr), :]
+            dst = far_ref.at[pl.ds(pl.multiple_of(r0 - core * TAIL - (N_D - 1) * PART + PART, LANES), nr), :]
         return pltpu.make_async_remote_copy(
             src_ref=view(b2, name, layer, r0, nr, c0, nc, False), dst_ref=dst,
             send_sem=s3s.at[slot], recv_sem=s3r.at[slot], device_id=c_dev, device_id_type=MESH)
@@ -323,14 +326,14 @@
         return pl.multiple_of(side_no * (2 * FF_ROWS) + 2560, HEAD)
 
     def tile_col(side_no, core_no, tile):
-        return pl.multiple_of(side_no * (2 * FF_ROWS) + core_no * (FF_ROWS + TAIL) + tile * 256, HEAD)
+        return pl.multiple_of(side_no * (2 * FF_ROWS) + core_no * (FF_ROWS + TAIL) + tile * PART, HEAD)
 
     def near_far():
-        r0 = pl.multiple_of(core * TAIL + (N_D - 1) * 256, 64)
-        return pltpu.make_async_copy(b2["d"].at[LAYERS - 1, pl.ds(r0, 256), :], far_ref.at[pl.ds(0, 256), :], lsem.at[0])
+        r0 = pl.multiple_of(core * TAIL + (N_D - 1) * PART, 64)
+        return pltpu.make_async_copy(b2["d"].at[LAYERS - 1, pl.ds(r0, PART), :], far_ref.at[pl.ds(0, PART), :], lsem.at[0])
 
     def near_rest():
-        r0 = pl.multiple_of((1 - core) * 2560, 512)
+        r0 = pl.multiple_of((1 - core) * 2560, WIDTH)
         return [pltpu.make_async_copy(b2["d"].at[LAYERS - 1, pl.ds(r0, TAIL), pl.ds(n * WIDE, WIDE)], rest_rows(n * WIDE), lsem.at[1 + n])
                 for n in range(2)]
 
@@ -346,22 +349,22 @@
 
         @pl.when(i == 0)
         def _():
-            cols("k", 0, 256, 0)
-            cols("v", 0, 256, 256)
+            cols("k", 0, PART, 0)
+            cols("v", 0, PART, PART)
 
         @pl.when((i >= ST_Q) & (i < ST_A))
         def _():
-            cols("q", pl.multiple_of((i - ST_Q) * 512, 512), 512, 0)
+            cols("q", pl.multiple_of((i - ST_Q) * WIDTH, WIDTH), WIDTH, 0)
 
         @pl.when((i >= ST_O) & (i < ST_G))
         def _():
-            cols("o", pl.multiple_of((i - ST_O) * 512, 512), 512, 0)
+            cols("o", pl.multiple_of((i - ST_O) * WIDTH, WIDTH), WIDTH, 0)
 
         @pl.when((i >= ST_G) & (i < ST_D))
         def _():
-            c0 = pl.multiple_of((i - ST_G) * 256, 256)
-            cols("g", c0, 256, 0)
-            cols("u", c0, 256, 256)
+            c0 = pl.multiple_of((i - ST_G) * PART, PART)
+            cols("g", c0, PART, 0)
+            cols("u", c0, PART, PART)
 
         j, tile, half, whole, near, far, rest = down_step(i)
         dslot = lax.rem(j + 2 * STEPS, 2)
@@ -371,16 +374,16 @@
 
         def chunk_rows(r, tile_no, w0):
             src_core = core if r % 2 == 0 else 1 - core
-            rows_in(sources[r], pl.multiple_of(src_core * TAIL + tile_no * 256, 64), 256, w0)
+            rows_in(sources[r], pl.multiple_of(src_core * TAIL + tile_no * PART, 64), PART, w0)
 
         def rest_rows(r, w0):
             src_core = core if r % 2 == 0 else 1 - core
-            rows_in(sources[r], pl.multiple_of((1 - src_core) * 2560, 512), TAIL, pl.multiple_of(w0 + src_core * TAIL, 64))
+            rows_in(sources[r], pl.multiple_of((1 - src_core) * 2560, WIDTH), TAIL, pl.multiple_of(w0 + src_core * TAIL, 64))
 
         @pl.when((whole & (half == 0) & (i != ST_READY + 1)) | (i == ST_READY))
         def _():
             for r in range(3):
-                chunk_rows(r, jnp.where(i == ST_READY, N_D - 2, tile), r * 256)
+                chunk_rows(r, jnp.where(i == ST_READY, N_D - 2, tile), r * PART)
 
         @pl.when(whole & (half == 0))
         def _():
@@ -389,13 +392,13 @@
         @pl.when(near & (half == 0))
         def _():
             for r in range(2):
-                chunk_rows(r, N_D - 1, r * 256)
-                rest_rows(r, 512)
+                chunk_rows(r, N_D - 1, r * PART)
+                rest_rows(r, WIDTH)
 
         @pl.when(far & (half == 0) & (layer < LAYERS - 1))
         def _():
             for r in range(2):
-                chunk_rows(2 + r, N_D - 1, r * 256)
+                chunk_rows(2 + r, N_D - 1, r * PART)
 
         @pl.when(far & (half == 0) & (layer == LAYERS - 1))
         def _():
@@ -436,35 +439,35 @@
         def fin(rows, acc):
             for b in range(2):
                 kv_ref[rows, pl.ds(b * HEAD, HEAD)] = rotate(acc[:, b * HEAD:(b + 1) * HEAD], rows)
-            kv_ref[rows, pl.ds(256, 256)] = acc[:, 256:].astype(BF16)
+            kv_ref[rows, pl.ds(PART, PART)] = acc[:, PART:].astype(BF16)
         tile_product(slot, fin)
 
     def q_step(slot, j):
         def fin(rows, acc):
             for b in range(4):
-                c0 = pl.multiple_of(j * 512 + b * HEAD, HEAD)
+                c0 = pl.multiple_of(j * WIDTH + b * HEAD, HEAD)
                 q_ref[rows, pl.ds(c0, HEAD)] = rotate(acc[:, b * HEAD:(b + 1) * HEAD], rows)
         tile_product(slot, fin)
 
     def o_step(slot, j):
         def fin(rows, acc):
-            c0 = pl.ds(pl.multiple_of(j * 512, 512), 512)
+            c0 = pl.ds(pl.multiple_of(j * WIDTH, WIDTH), WIDTH)
             x_ref[rows, c0] = x_ref[rows, c0] + acc
         tile_product(slot, fin)
 
     def g_step(slot, j):
         def fin(rows, acc):
-            gate = acc[:, :256]
-            up = acc[:, 256:]
-            c0 = pl.multiple_of(j * 256, 256)
-            a_ref[rows, pl.ds(c0, 256)] = (gate * jax.nn.sigmoid(gate) * up).astype(BF16)
+            gate = acc[:, :PART]
+            up = acc[:, PART:]
+            c0 = pl.multiple_of(j * PART, PART)
+            a_ref[rows, pl.ds(c0, PART)] = (gate * jax.nn.sigmoid(gate) * up).astype(BF16)
         tile_product(slot, fin)
 
     def attend(head):
         kv = head // 8
         q0 = pl.multiple_of(head * HEAD, HEAD)
         k0 = pl.multiple_of(kv * HEAD, HEAD)
-        v0 = pl.multiple_of(256 + kv * HEAD, HEAD)
+        v0 = pl.multiple_of(PART + kv * HEAD, HEAD)
         o0 = pl.multiple_of(rel(head // 4) * ROWS + lax.rem(head, 4) * HEAD, HEAD)
         scale = HEAD ** -0.5
         for b in range(TOK // QB):
@@ -498,7 +501,7 @@
             pltpu.make_async_copy(part, part, dsem.at[dslot]).wait()
 
     def last_cols(side_no):
-        return [(tile_col(side_no, core, N_D - 1), 256), (tile_col(side_no, 1 - core, N_D - 1), 256)]
+        return [(tile_col(side_no, core, N_D - 1), PART), (tile_col(side_no, 1 - core, N_D - 1), PART)]
 
     def wait_w(slot):
         pltpu.make_async_copy(wbuf.at[slot], wbuf.at[slot], wsem.at[slot]).wait()
@@ -553,7 +556,7 @@
         @pl.when(whole)
         def _():
             wait_d(dslot, half, 1024)
-            add_product(dslot, half, [(tile_col(lax.rem(side + r // 2, 2), lax.rem(core + r, 2), tile), 256) for r in range(4)])
+            add_product(dslot, half, [(tile_col(lax.rem(side + r // 2, 2), lax.rem(core + r, 2), tile), PART) for r in range(4)])
 
         @pl.when(near)
         def _():
@@ -562,7 +565,7 @@
 
         @pl.when(far & (layer < LAYERS - 1))
         def _():
-            wait_d(dslot, half, 512)
+            wait_d(dslot, half, WIDTH)
             add_product(dslot, half, last_cols(1 - side))
 
         @pl.when(far & (layer == LAYERS - 1))
@@ -594,20 +597,20 @@
         for layer in range(LAYERS):
             gain_ref[n * LAYERS + layer] = ref[pl.ds(layer, 1), :].astype(F32)
     ids = seg_ref[...].astype(F32)
-    lane = lax.broadcasted_iota(jnp.int32, (128, HEAD), 1)
-    for b in range(TOK // 128):
-        rows = pl.ds(b * 128, 128)
-        mine = jnp.transpose(jnp.broadcast_to(ids[b:b + 1, :], (128, 128)))
-        before = jnp.zeros((128, 128), F32)
-        for c in range(TOK // 128):
+    lane = lax.broadcasted_iota(jnp.int32, (LANES, HEAD), 1)
+    for b in range(TOK // LANES):
+        rows = pl.ds(b * LANES, LANES)
+        mine = jnp.transpose(jnp.broadcast_to(ids[b:b + 1, :], (LANES, LANES)))
+        before = jnp.zeros((LANES, LANES), F32)
+        for c in range(TOK // LANES):
             before = before + jnp.where(ids[c:c + 1, :] < mine, 1.0, 0.0)
         first = jnp.sum(before, axis=1, keepdims=True)
-        pos = lax.broadcasted_iota(jnp.int32, (128, 128), 0).astype(F32) + (b * 128.0) - first
+        pos = lax.broadcasted_iota(jnp.int32, (LANES, LANES), 0).astype(F32) + (b * 128.0) - first
         angles = pos * freq_ref[...]
         cos_ref[rows, :] = jnp.cos(angles)
         sin = jnp.sin(angles)
         sin_ref[rows, :] = jnp.where(lane < HEAD // 2, -sin, sin)
-        first_ref[rows, :] = jnp.broadcast_to(first, (128, 128)).astype(jnp.int32)
+        first_ref[rows, :] = jnp.broadcast_to(first, (LANES, LANES)).astype(jnp.int32)
 
     @pl.loop(0, TOK // NB)
     def _(m):
@@ -639,14 +642,14 @@
     c0 = pl.multiple_of((1 - lax.axis_index("fsdp") // 2) * (2 * FF_ROWS) + 2560, HEAD)
 
     def store(n, m):
-        rows, cols = pl.ds(m * 512, 512), pl.ds(n * 512, 512)
+        rows, cols = pl.ds(m * WIDTH, WIDTH), pl.ds(n * WIDTH, WIDTH)
         return pltpu.make_async_copy(y_ref.at[rows, cols], out.at[rows, cols], osem.at[n, m])
 
     for n in range(4):
-        cols = pl.ds(n * 512, 512)
-        tile = a_ref[pl.ds(n // 2 * REST_K, REST_K), pl.ds(FF + n % 2 * 512, 512)]
+        cols = pl.ds(n * WIDTH, WIDTH)
+        tile = a_ref[pl.ds(n // 2 * REST_K, REST_K), pl.ds(FF + n % 2 * WIDTH, WIDTH)]
         for m in range(2):
-            rows = pl.ds(m * 512, 512)
+            rows = pl.ds(m * WIDTH, WIDTH)
             y_ref[rows, cols] = x_ref[rows, cols] + jnp.dot(a_ref[rows, pl.ds(c0, REST_K)], tile, preferred_element_type=F32)
             store(n, m).start()
     for n in range(4):
@@ -671,18 +674,18 @@
         scratch_shapes=[
             pltpu.VMEM((TOK, D), BF16),
             pltpu.VMEM((TOK, D), BF16),
-            pltpu.VMEM((TOK, 512), BF16),
-            pltpu.VMEM((2, D, 512), BF16),
+            pltpu.VMEM((TOK, WIDTH), BF16),
+            pltpu.VMEM((2, D, WIDTH), BF16),
             pltpu.VMEM((2, 1024, D), BF16),
             pltpu.VMEM((TOK, HEAD), F32),
             pltpu.VMEM((TOK, HEAD), F32),
             pltpu.VMEM((TOK, HEAD), jnp.int32),
             pltpu.VMEM((2 * LAYERS, 1, D), F32),
-            pltpu.VMEM((TOK // 128, 128), jnp.int32),
+            pltpu.VMEM((TOK // LANES, LANES), jnp.int32),
             pltpu.VMEM((1, HEAD), F32),
             pltpu.VMEM((LAYERS, D), BF16),
             pltpu.VMEM((LAYERS, D), BF16),
-            pltpu.VMEM((512, D), BF16),
+            pltpu.VMEM((WIDTH, D), BF16),
             pltpu.SemaphoreType.DMA((2,)),
             pltpu.SemaphoreType.DMA((2,)),
             pltpu.SemaphoreType.DMA((5,)),
@@ -690,7 +693,7 @@
         ] + [sem] * 2 + [item_sem] * 4 + [sem] * 2,
         compiler_params=pltpu.CompilerParams(collective_id=0, has_side_effects=True, vmem_limit_bytes=32 * 1000 * 1000),
         name="two_layers",
-    )(tokens, seg_ids.reshape(TOK // 128, 128), freq, g_attn, g_mlp, *weights)
+    )(tokens, seg_ids.reshape(TOK // LANES, LANES), freq, g_attn, g_mlp, *weights)
     hidden = pltpu.with_memory_space_constraint(outs[0], pltpu.VMEM)
     act = pltpu.with_memory_space_constraint(outs[1], pltpu.VMEM)
     return pl.pallas_call(

time: 844 us -> 844 us (level)
  no operation moved by 1% of the time
where the time goes in v3:
time: 844 us
  Pallas kernels  844 us (100%)
    pallas_call x1, Pallas kernels, run_layers(): pl.pallas_call(layer_kernel, out_shape=[pltpu.VMEM((TOK, D), F32), pltpu....  840 us

profile of v3, /device:TPU:0, one launch (start us, length us, event | category | flops | bytes accessed | tf_op | source)
XLA Modules:
  0.0 843.9 jit_solution(8806825129882852611)
XLA Ops:
  0.0 839.9 %two_layers.1 = (f32[1024,2048]{1,0:T(8,128)S(1)}, bf16[1024,12032]{1,0:T(8,128)(2,1)S(1)}, bf16[2,512,2048]{2,1,0:T(8,128)(2,1)}, bf16[2,512,256]{2,1,0:T(8,128...) custom-call(bf16[1024,2048]{1,0:T(8,128)(2,1)} %refs_0_.1, ...), custom_call_target="tpu_custom_call" | custom-call | tf_op jit(solution)/shard_map/two_layers/pallas_call | solution.py:669
  839.9 3.8 result.1

commit v4 on v3

--- a/solution.py
+++ b/solution.py
@@ -266,10 +266,10 @@
         final = i == STEPS - 1
         t3 = jnp.where(i < ST_D, jnp.where(i < ST_A, 3 + i, (t2 - 3) // 2),
              jnp.where(first, jnp.where(i < ST_IDLE, (t2 - 2) // 2, CH_DR + (i - ST_IDLE + 1) // 2 + jnp.where(final, 1, 0)),
-             jnp.where(i < ST_READY - 4, (t2 - 2) // 2, jnp.where(i < ST_READY + 2, 39 + (i - ST_READY + 4) // 3, i - ST_READY + 39 + jnp.where(i == ST_FAR, 1, 0)))))
-        end = s >= ALL_STEPS - 2
+             jnp.where(i < ST_READY - 4, (t2 - 2) // 2, jnp.where(i < ST_READY + 2, 39 + (i - ST_READY + 4) // 3, i - ST_READY + 39))))
+        end = s >= ALL_STEPS - 1
         t2 = jnp.minimum(t2 + layer * 2 * PER_LAYER, jnp.where(end, ITEMS, ITEMS - 1))
-        t3 = jnp.minimum(t3 + layer * PER_LAYER, PUSHES)
+        t3 = jnp.minimum(t3 + layer * PER_LAYER, jnp.where(end, PUSHES, PUSHES - 1))
         nxt = jnp.minimum(s + 1, ALL_STEPS - 1)
         i = lax.rem(nxt, STEPS)
         base = nxt // STEPS * PER_LAYER
@@ -304,6 +304,11 @@
                 k = p - jnp.minimum(extra, 1)
                 part = jnp.where((p < CHUNKS - 2) | (extra > 1), 2, extra)
                 for_pair(k, arrived, part)
+
+                @pl.when(p == CHUNKS - 1)
+                def _():
+                    near_far().start()
+
                 for_chunk(k, relay3, 3, part)
                 for_chunk(jnp.where(part == 1, CHUNKS, k), pushed)
 
@@ -399,10 +404,6 @@
         def _():
             for r in range(2):
                 chunk_rows(2 + r, N_D - 1, r * PART)
-
-        @pl.when(far & (half == 0) & (layer == LAYERS - 1))
-        def _():
-            near_far().start()
 
         @pl.when(rest & (half == 0))
         def _():
@@ -573,6 +574,9 @@
             @pl.when(half == 0)
             def _():
                 near_far().wait()
+
+            @pl.when(half == 1)
+            def _():
                 for copy in near_rest():
                     copy.start()
             add_product(dslot, half, last_cols(1 - side), far_ref)

time: 844 us -> 844 us (level)
  no operation moved by 1% of the time
where the time goes in v4:
time: 844 us
  Pallas kernels  844 us (100%)
    pallas_call x1, Pallas kernels, run_layers(): pl.pallas_call(layer_kernel, out_shape=[pltpu.VMEM((TOK, D), F32), pltpu....  840 us

profile of v4, /device:TPU:0, one launch (start us, length us, event | category | flops | bytes accessed | tf_op | source)
XLA Modules:
  0.0 843.8 jit_solution(773327430113160314)
XLA Ops:
  0.0 839.8 %two_layers.1 = (f32[1024,2048]{1,0:T(8,128)S(1)}, bf16[1024,12032]{1,0:T(8,128)(2,1)S(1)}, bf16[2,512,2048]{2,1,0:T(8,128)(2,1)}, bf16[2,512,256]{2,1,0:T(8,128...) custom-call(bf16[1024,2048]{1,0:T(8,128)(2,1)} %refs_0_.1, ...), custom_call_target="tpu_custom_call" | custom-call | tf_op jit(solution)/shard_map/two_layers/pallas_call | solution.py:673
  839.8 3.8 result.1
